TPU v7x, 32 devices: a whole 2x2x4 slice. The times are simulated.
32 devices in a mesh: expert: 4 (over y, x), shard: 8 (over z, core).
Axes of the slice: x: 2, y: 2, z: 4, core: 2. Of those that a mesh axis runs over, the one named last changes fastest.
Arguments:
- tokens: bfloat16 [256, 6144], P(('expert', 'shard')), may hold values from -6 to 6
- norm_gain: float32 [6144], replicated, may hold values from 0.5 to 1.5
- routes: int32 [256, 2], P(('expert', 'shard')), may hold values from 0 to 3, all different within a row; in each aligned block of 8 rows (0 to 7, 8 to 15, ...) at most 4 rows name the same one
- gate_weights: float32 [256, 2], P(('expert', 'shard')), may hold values from 0.2 to 1
- capacity: int32 [4], replicated, may hold values from 2 to 4
- w_gate: bfloat16 [4, 6144, 8192], P('expert', None, 'shard'), may hold values from -0.078125 to 0.078125
- w_up: bfloat16 [4, 6144, 8192], P('expert', None, 'shard'), may hold values from -0.078125 to 0.078125
- w_down: bfloat16 [4, 8192, 6144], P('expert', 'shard'), may hold values from -0.0625 to 0.0625
Outputs:
- mixed_out: bfloat16 [256, 6144], P(('expert', 'shard'))
Inputs may be any that keep to these rules, and one draw needn't show every extreme that they name: `routes`: each row names 2 different experts; among the rows of one device no expert is named by more than 4 rows.
All inputs are finite; a program needn't handle non-finite values.
Results may differ from a plain program's by a relative error of at most 0.019.
Values may be sent and summed in bfloat16 or wider, within the bound.
A program may use at most 128 MiB of HBM per device.

v0:
```python
import jax
import jax.numpy as jnp
from jax import lax
from jax.sharding import PartitionSpec as P


def rms_norm(tokens, norm_gain):
    widened = tokens.astype(jnp.float32)
    mean_square = jnp.mean(widened * widened, axis=-1, keepdims=True)
    return (widened * lax.rsqrt(mean_square + 1e-05) * norm_gain).astype(jnp.bfloat16)


def slot_ranks(blocked):
    equal_ids = blocked[:, :, None, :, None] == blocked[:, None, :, None, :]
    shared = jnp.any(equal_ids, axis=4).astype(jnp.int32)
    per_block = blocked.shape[1]
    positions = jnp.arange(per_block, dtype=jnp.int32)
    earlier = (positions[None, :] < positions[:, None]).astype(jnp.int32)
    return jnp.sum(shared * earlier[None, :, :, None], axis=2)


def on_device(tokens, norm_gain, routes, gate_weights, capacity, w_gate, w_up, w_down):
    normed = rms_norm(tokens, norm_gain)
    tok_count = tokens.shape[0]
    expert_count = capacity.shape[0]
    slot_depth = max(tok_count // 2, tok_count * routes.shape[1] // expert_count)
    slot_rank = slot_ranks(routes[None])[0]
    expert_ids = jnp.arange(expert_count, dtype=jnp.int32)
    is_expert = routes[:, :, None] == expert_ids
    limit_rows = jnp.sum(jnp.where(is_expert, capacity, 0), axis=-1)
    kept_mask = slot_rank < limit_rows
    slot_ids = jnp.arange(slot_depth, dtype=jnp.int32)
    matched = (
        is_expert[:, :, :, None]
        & (slot_rank[:, :, None, None] == slot_ids)
        & kept_mask[:, :, None, None]
    )
    picker = jnp.sum(matched.astype(jnp.float32), axis=1).astype(jnp.bfloat16)
    buffers = jnp.einsum("tej,td->ejd", picker, normed, preferred_element_type=jnp.float32).astype(
        jnp.bfloat16
    )
    combine = jnp.sum(jnp.where(matched, gate_weights[:, :, None, None], jnp.float32(0.0)), axis=1)
    gate_proj = w_gate[0]
    up_proj = w_up[0]
    down_proj = w_down[0]
    arrived = lax.all_to_all(buffers, "expert", split_axis=0, concat_axis=0, tiled=True)
    slot_rows = lax.all_gather(arrived[None], "shard", axis=0, tiled=True)
    row_shape = slot_rows.shape
    flat_rows = slot_rows.reshape(-1, row_shape[-1])
    gate_val = jnp.dot(flat_rows, gate_proj, preferred_element_type=jnp.float32)
    up_val = jnp.dot(flat_rows, up_proj, preferred_element_type=jnp.float32)
    hidden = (jax.nn.silu(gate_val) * up_val).astype(jnp.bfloat16)
    partial_out = jnp.dot(hidden, down_proj, preferred_element_type=jnp.float32)
    partial_value = partial_out.reshape(row_shape[:-1] + (down_proj.shape[1],))
    rounded_parts = partial_value.astype(jnp.bfloat16)
    pieces = lax.all_to_all(
        lax.all_to_all(rounded_parts, "expert", split_axis=1, concat_axis=1, tiled=True),
        "shard",
        split_axis=0,
        concat_axis=0,
        tiled=True,
    )
    returned = jnp.sum(pieces.astype(jnp.float32), axis=0).astype(jnp.bfloat16)
    mixed_out = jnp.einsum(
        "tej,ejd->td", combine, returned.astype(jnp.float32), precision=lax.Precision.HIGHEST
    )
    return mixed_out.astype(jnp.bfloat16)


def solution(mesh):
    in_specs = (
        P(("expert", "shard"), None),
        P(),
        P(("expert", "shard"), None),
        P(("expert", "shard"), None),
        P(),
        P("expert", None, "shard"),
        P("expert", None, "shard"),
        P("expert", "shard", None),
    )
    out_specs = P(("expert", "shard"), None)
    return jax.shard_map(
        on_device, mesh=mesh, in_specs=in_specs, out_specs=out_specs, check_vma=False
    )
```

profile of v0, /device:TPU:0, one launch (start us, length us, event | category | flops | bytes accessed | tf_op | source)
XLA Modules:
  0.0 144.9 jit_solution(16787414954088235093)
XLA Ops:
  6.5 0.0 all-gather.3.cloned.1.call-start
  6.5 1.1 fusion.17
  7.6 0.8 compare_reduce_fusion
  8.4 0.8 select_reduce_fusion.2
  9.2 0.1 select_reduce_fusion.1
  9.4 0.7 iota_compare_fusion
  10.1 0.7 convert_reduce_fusion
  10.8 1.1 convolution_convert_fusion
  11.9 10.6 %all_to_all.15 = bf16[4,4,6144]{2,1,0:T(4,128)(2,1)} all-to-all(bf16[4,4,6144]{2,1,0:T(4,128)(2,1)S(1)} %convolution_convert_fusion), channel_id=1, replica_groups=mesh['expert'=4,'shard'=8] {'expert'}, dimensions={0} | all-to-all | bytes 393216 | tf_op jit(solution)/shard_map/all_to_all | solution.py:46
  22.6 0.0 all-gather.3.cloned.1.call-update
  22.6 25.0 %all-gather.3.cloned.1.call-done = bf16[32,4,6144]{2,1,0:T(4,128)(2,1)} async-done(((bf16[4,4,6144]{2,1,0:T(4,128)(2,1)}), bf16[32,4,6144]{2,1,0:T(4,128)(2,1)}) %all-gather.3.cloned.1.call-update) | async-done | bytes 1572880 | tf_op jit(solution)/shard_map/all_gather | solution.py:47
  47.6 2.7 %reshape.66 = bf16[128,6144]{1,0:T(8,128)(2,1)S(1)} reshape(bf16[32,4,6144]{2,1,0:T(4,128)(2,1)} %all-gather.3.cloned.1.call-done) | data formatting | bytes 3145728 | tf_op jit(solution)/shard_map/reshape | solution.py:49
  50.3 6.5 %fusion.4 = f32[128,1024]{1,0:T(8,128)S(1)} fusion(bf16[128,6144]{1,0:T(8,128)(2,1)S(1)} %reshape.66, bf16[1,6144,1024]{2,1,0:T(8,128)(2,1)} %param.13), kind=kOutput, calls=%fused_computation.4 | convolution fusion | flops 1610612736 | bytes 14680064 | tf_op jit(solution)/shard_map/dot_general | solution.py:50
  56.8 6.6 %fusion.13 = bf16[128,1024]{1,0:T(8,128)(2,1)S(1)} fusion(bf16[128,6144]{1,0:T(8,128)(2,1)S(1)} %reshape.66, bf16[1,6144,1024]{2,1,0:T(8,128)(2,1)} %param.14, f32[128,1024]{1,0:T(8,128)S(1)} %fusion.4), kind=kOutput, calls=%fused_computation.11 | convolution fusion | flops 1611399168 | bytes 14942208 | tf_op jit(solution)/shard_map/dot_general | solution.py:51
  63.3 0.1 dot_general.20
  63.4 7.9 %fusion.6 = bf16[8,4,4,6144]{3,2,0,1:T(4,128)(2,1)S(1)} fusion(bf16[1,1024,6144]{2,1,0:T(8,128)(2,1)} %param.15, bf16[8,4,4,1024]{3,2,1,0:T(4,128)(2,1)S(1)} %dot_general.20), kind=kOutput, calls=%fused_computation.6 | convolution fusion | flops 1611399168 | bytes 14417920 | tf_op jit(solution)/shard_map/dot_general | solution.py:53
  71.4 23.6 %all_to_all.16 = bf16[8,4,4,6144]{3,2,0,1:T(4,128)(2,1)S(1)} all-to-all(bf16[8,4,4,6144]{3,2,0,1:T(4,128)(2,1)S(1)} %fusion.6), channel_id=1, replica_groups=mesh['expert'=4,'shard'=8] {'expert'}, dimensions={1} | all-to-all | bytes 3145728 | tf_op jit(solution)/shard_map/all_to_all | solution.py:57
  95.0 0.7 copy.24
  95.7 40.4 %all_to_all.17 = bf16[8,4,4,6144]{3,2,1,0:T(4,128)(2,1)S(1)} all-to-all(bf16[8,4,4,6144]{3,2,1,0:T(4,128)(2,1)S(1)} %copy.24), channel_id=1, replica_groups=mesh['expert'=4,'shard'=8] {'shard'}, dimensions={0} | all-to-all | bytes 3145728 | tf_op jit(solution)/shard_map/all_to_all | solution.py:56
  136.1 0.9 reduce_sum.62
  137.0 1.0 fusion.9
  (3 shorter events, 0.0 us)
Async XLA Ops:
  6.5 41.0 %all-gather.3.cloned.1.call-start = ((), (), s32[]{:S(2)}) async-start(), calls=%async_computation.3 | async-start | bytes 1769472 | tf_op jit(solution)/shard_map/all_gather | solution.py:47
Sparse Core Ops, SparseCore 0:
  22.7 24.7 all-gather.2
where the time goes:
time: 145 us
  blocking collectives  74.7 us (52%)
  waiting for transfers between devices  25 us (17%)
  matrix products  23.1 us (16%)
  between operations  13.5 us (9%)
  other arithmetic  5.17 us (4%)
  local copies, waits for them, and re-layouts  3.49 us (2%)
    all_to_all x1, blocking collectives, on_device(): lax.all_to_all(lax.all_to_all(rounded_parts, 'expert', split_axis=1, conc...  40.4 us
    all_gather x1, waiting for transfers between devices, on_device(): slot_rows = lax.all_gather(arrived[None], 'shard', axis=0, tiled=True)  25 us
    all_to_all x1, blocking collectives, on_device(): lax.all_to_all(rounded_parts, 'expert', split_axis=1, concat_axis=1, tile...  23.6 us
    all_to_all x1, blocking collectives, on_device(): lax.all_to_all(buffers, 'expert', split_axis=0, concat_axis=0, tiled=True)  10.6 us
    dot_general x1, matrix products, on_device(): partial_out = jnp.dot(hidden, down_proj, preferred_element_type=jnp.float32)  7.91 us
    dot_general x1, matrix products, on_device(): up_val = jnp.dot(flat_rows, up_proj, preferred_element_type=jnp.float32)  6.57 us
    dot_general x1, matrix products, on_device(): gate_val = jnp.dot(flat_rows, gate_proj, preferred_element_type=jnp.float32)  6.49 us
  transfers between devices with their start and end apart: 1, of which 1 were waited for; matrix products, arithmetic and copies ran while one was open for 0% of the time, Pallas kernels for 0%

commit v1 on v0

v1 whole, which is shorter than its diff:
```python
import functools

import jax
import jax.numpy as jnp
from jax import lax
from jax.experimental import pallas as pl
from jax.experimental.pallas import tpu as pltpu
from jax.sharding import PartitionSpec as P

CHUNKS = 4
EPS = 1e-05
MESH = pl.DeviceIdType.MESH
CORES = 2


def column_tile(width, most):
    tile = most
    while width % tile:
        tile //= 2
    return tile


def kernel(
    n_expert, n_line, depth,
    tokens, gain, routes, gates, capacity, gate_hbm, up_hbm, down_hbm, out,
    gate_w, up_w, down_w, meta, normed, picked, rows, acc_gate, acc_up, hidden, partner, summed, returned, mixed, final,
    w_sem, meta_send, meta_recv, line_send, line_recv, plane_send, plane_recv, relay_send, relay_recv,
    pair_send, pair_recv, back_send, back_recv, home_send, home_recv,
):
    expert = lax.axis_index("expert")
    shard = lax.axis_index("shard")
    place, core = shard // CORES, lax.rem(shard, CORES)
    other = 1 - core
    tok, width = tokens.shape
    cols = width // CHUNKS
    slots = n_line * depth
    used = n_expert * slots
    lanes = meta.shape[2]
    hid = gate_w.shape[1]
    total_rows = CORES * used

    def line_at(step):
        return lax.rem(place + step + n_line, n_line)

    def expert_at(step):
        return lax.rem(expert + step + n_expert, n_expert)

    def line_device(step):
        return {"expert": expert, "shard": line_at(step) * CORES + core}

    def plane_device(step):
        return {"expert": expert_at(step), "shard": shard}

    partner_device = {"expert": expert, "shard": place * CORES + other}
    peers = [line_device(d) for d in range(1, n_line)] + [plane_device(d) for d in range(1, n_expert)] + [partner_device]

    barrier = pltpu.get_barrier_semaphore()
    for peer in peers:
        pl.semaphore_signal(barrier, inc=1, device_id=peer, device_id_type=MESH)

    def weight_copy(kind, step):
        span = pl.ds(step * cols, cols)
        if kind == 0:
            return pltpu.make_async_copy(gate_hbm.at[0, span, :], gate_w.at[span, :], w_sem.at[0, step])
        if kind == 1:
            return pltpu.make_async_copy(up_hbm.at[0, span, :], up_w.at[span, :], w_sem.at[1, step])
        return pltpu.make_async_copy(down_hbm.at[0, :, span], down_w.at[:, span], w_sem.at[2, step])

    for step in range(CHUNKS):
        weight_copy(0, step).start()
        weight_copy(1, step).start()
    for step in range(CHUNKS):
        weight_copy(2, step).start()

    lane = lax.broadcasted_iota(jnp.int32, (tok, lanes), 1)
    row = lax.broadcasted_iota(jnp.int32, (tok, lanes), 0)
    lane_expert = lane // slots
    lane_slot = lax.rem(lane, depth)
    first = routes[:, 0:1] == lane_expert
    named = first.astype(jnp.float32)
    weight = jnp.where(first, gates[:, 0:1], 0.0)
    for k in range(1, routes.shape[1]):
        this = routes[:, k : k + 1] == lane_expert
        named = jnp.maximum(named, this.astype(jnp.float32))
        weight = jnp.where(this, gates[:, k : k + 1], weight)
    rank = jnp.zeros((tok, lanes), jnp.float32)
    for t in range(tok - 1):
        rank = rank + jnp.where(row > t, named[t : t + 1, :], 0.0)
    limit = jnp.zeros((tok, lanes), jnp.int32)
    for e in range(n_expert):
        limit = jnp.where(lane_expert == e, capacity[e], limit)
    rank = rank.astype(jnp.int32)
    keep = (named > 0.0) & (rank == lane_slot) & (rank < limit)
    meta[place] = jnp.where(keep, weight, 0.0)

    wide = tokens[...].astype(jnp.float32)
    scale = lax.rsqrt(jnp.mean(wide * wide, axis=-1, keepdims=True) + EPS)
    values = (wide * scale * gain[...]).astype(jnp.bfloat16)
    for step in range(CHUNKS):
        normed[step, place] = values[:, step * cols : (step + 1) * cols]

    pl.semaphore_wait(barrier, len(peers))
    sent = []

    def remote(src, dst, send, recv, device):
        return pltpu.make_async_remote_copy(
            src_ref=src, dst_ref=dst, send_sem=send, recv_sem=recv, device_id=device, device_id_type=MESH
        )

    def send(*args):
        copy = remote(*args)
        copy.start()
        return copy

    for d in range(1, n_line):
        sent.append(send(meta.at[place], meta.at[place], meta_send.at[d - 1], meta_recv.at[d - 1], line_device(d)))
    for step in range(CHUNKS):
        for d in range(1, n_line):
            block = normed.at[step, place]
            sent.append(send(block, block, line_send.at[step, d - 1], line_recv.at[step, d - 1], line_device(d)))
    for d in range(1, n_line):
        block = meta.at[line_at(-d)]
        remote(block, block, meta_send.at[d - 1], meta_recv.at[d - 1], line_device(-d)).wait_recv()

    tall = n_line * tok
    all_meta = meta[...].reshape(tall, lanes)
    lane = lax.broadcasted_iota(jnp.int32, (tall, lanes), 1)
    row = lax.broadcasted_iota(jnp.int32, (tall, lanes), 0)
    combine = jnp.where(lax.rem(lane // depth, n_line) == row // tok, all_meta, 0.0)
    picker = (combine != 0.0).astype(jnp.float32).T[:used].astype(jnp.bfloat16)
    combine = combine.astype(jnp.bfloat16)[:, :used]

    tile = column_tile(cols, 512)
    relays = []

    def pick(step):
        for d in range(1, n_line):
            block = normed.at[step, line_at(-d)]
            remote(block, block, line_send.at[step, d - 1], line_recv.at[step, d - 1], line_device(-d)).wait_recv()

        def body(i, _):
            span = pl.ds(pl.multiple_of(i * tile, tile), tile)
            gathered = normed[step, :, :, span].astype(jnp.float32).reshape(tall, tile).astype(jnp.bfloat16)
            chosen = jnp.dot(picker, gathered, preferred_element_type=jnp.float32)
            picked[step, :, :, span] = chosen.astype(jnp.bfloat16).reshape(n_expert, slots, tile)
            return 0

        lax.fori_loop(0, cols // tile, body, 0)
        for d in range(1, n_expert):
            sent.append(
                send(
                    picked.at[step, expert_at(d)], rows.at[step, core, expert],
                    plane_send.at[step, d - 1], plane_recv.at[step, d - 1], plane_device(d),
                )
            )
        rows[step, core, expert] = picked[step, expert]
        block = rows.at[step, core, expert]
        relays.append(send(picked.at[step, expert], block, relay_send.at[step, 0], relay_recv.at[step, 0], partner_device))

    def relay(step):
        for d in range(1, n_expert):
            block = rows.at[step, core, expert_at(-d)]
            remote(block, block, plane_send.at[step, d - 1], plane_recv.at[step, d - 1], plane_device(-d)).wait_recv()
            relays.append(send(block, block, relay_send.at[step, d], relay_recv.at[step, d], partner_device))

    hid_tile = column_tile(hid, 256)

    def project(step):
        for d in range(n_expert):
            block = rows.at[step, other, expert_at(-d)]
            remote(block, block, relay_send.at[step, d], relay_recv.at[step, d], partner_device).wait_recv()
        weight_copy(0, step).wait()
        weight_copy(1, step).wait()

        def body(i, _):
            span = pl.ds(pl.multiple_of(i * hid_tile, hid_tile), hid_tile)
            x = rows[step].reshape(total_rows, cols)
            depth_span = pl.ds(step * cols, cols)
            g = jnp.dot(x, gate_w[depth_span, span], preferred_element_type=jnp.float32)
            u = jnp.dot(x, up_w[depth_span, span], preferred_element_type=jnp.float32)
            if step > 0:
                g = g + acc_gate[:, span]
                u = u + acc_up[:, span]
            if step < CHUNKS - 1:
                acc_gate[:, span] = g
                acc_up[:, span] = u
            else:
                hidden[:, span] = (g / (1.0 + jnp.exp(-g)) * u).astype(jnp.bfloat16)
            return 0

        lax.fori_loop(0, hid // hid_tile, body, 0)

    for i in range(CHUNKS + 2):
        if i < CHUNKS:
            pick(i)
        if 0 <= i - 1 < CHUNKS:
            relay(i - 1)
        if 0 <= i - 2 < CHUNKS:
            project(i - 2)
    for copy in relays:
        copy.wait_send()

    def down(step):
        weight_copy(2, step).wait()

        def body(i, _):
            span = pl.ds(pl.multiple_of(i * tile, tile), tile)
            w_span = pl.ds(pl.multiple_of(step * cols + i * tile, tile), tile)
            y = jnp.dot(hidden[...], down_w[:, w_span], preferred_element_type=jnp.float32)
            rows[step, :, :, :, span] = y.astype(jnp.bfloat16).reshape(CORES, n_expert, slots, tile)
            return 0

        lax.fori_loop(0, cols // tile, body, 0)
        sent.append(send(rows.at[step, other], partner.at[step], pair_send.at[step], pair_recv.at[step], partner_device))

    def pair(step):
        remote(rows.at[step, core], partner.at[step], pair_send.at[step], pair_recv.at[step], partner_device).wait_recv()
        for d in range(n_expert):
            e = expert_at(d)
            both = rows[step, core, e].astype(jnp.float32) + partner[step, e].astype(jnp.float32)
            if d == 0:
                returned[step, e] = both.astype(jnp.bfloat16)
            else:
                summed[step, e] = both.astype(jnp.bfloat16)
                sent.append(
                    send(
                        summed.at[step, e], returned.at[step, expert],
                        back_send.at[step, d - 1], back_recv.at[step, d - 1], plane_device(d),
                    )
                )

    def mix(step):
        for d in range(1, n_expert):
            block = returned.at[step, expert_at(-d)]
            remote(block, block, back_send.at[step, d - 1], back_recv.at[step, d - 1], plane_device(-d)).wait_recv()

        def body(i, _):
            span = pl.ds(pl.multiple_of(i * tile, tile), tile)
            r = returned[step, :, :, span].reshape(used, tile)
            o = jnp.dot(combine, r, preferred_element_type=jnp.float32)
            mixed[step, :, :, span] = o.reshape(n_line, tok, tile).astype(jnp.bfloat16)
            return 0

        lax.fori_loop(0, cols // tile, body, 0)
        for d in range(1, n_line):
            sent.append(
                send(
                    mixed.at[step, line_at(d)], final.at[step, place],
                    home_send.at[step, d - 1], home_recv.at[step, d - 1], line_device(d),
                )
            )

    def finish(step):
        total = mixed[step, place].astype(jnp.float32)
        for d in range(1, n_line):
            block = final.at[step, line_at(-d)]
            remote(block, block, home_send.at[step, d - 1], home_recv.at[step, d - 1], line_device(-d)).wait_recv()
        for d in range(1, n_line):
            total = total + final[step, line_at(-d)].astype(jnp.float32)
        out[:, step * cols : (step + 1) * cols] = total.astype(jnp.bfloat16)

    for i in range(CHUNKS + 1):
        if i < CHUNKS:
            down(i)
        if 0 <= i - 1 < CHUNKS:
            pair(i - 1)
    for i in range(CHUNKS):
        mix(i)
    for i in range(CHUNKS):
        finish(i)
    for copy in sent:
        copy.wait_send()


def solution(mesh):
    n_expert = mesh.shape["expert"]
    n_line = mesh.shape["shard"] // CORES

    def on_device(tokens, norm_gain, routes, gate_weights, capacity, w_gate, w_up, w_down):
        tok, width = tokens.shape
        hid = w_gate.shape[2]
        depth = max(tok // 2, tok * routes.shape[1] // n_expert)
        cols = width // CHUNKS
        slots = n_line * depth
        used = n_expert * slots
        lanes = -(-used // 128) * 128
        dma = pltpu.SemaphoreType.DMA
        bf16 = jnp.bfloat16
        vmem = pl.BlockSpec(memory_space=pltpu.VMEM)
        hbm = pl.BlockSpec(memory_space=pl.ANY)
        line, plane = (CHUNKS, n_line - 1), (CHUNKS, n_expert - 1)
        return pl.pallas_call(
            functools.partial(kernel, n_expert, n_line, depth),
            out_shape=jax.ShapeDtypeStruct((tok, width), bf16),
            in_specs=[vmem, vmem, vmem, vmem, pl.BlockSpec(memory_space=pltpu.SMEM), hbm, hbm, hbm],
            out_specs=vmem,
            scratch_shapes=[
                pltpu.VMEM((width, hid), bf16),
                pltpu.VMEM((width, hid), bf16),
                pltpu.VMEM((hid, width), bf16),
                pltpu.VMEM((n_line, tok, lanes), jnp.float32),
                pltpu.VMEM((CHUNKS, n_line, tok, cols), bf16),
                pltpu.VMEM((CHUNKS, n_expert, slots, cols), bf16),
                pltpu.VMEM((CHUNKS, CORES, n_expert, slots, cols), bf16),
                pltpu.VMEM((CORES * used, hid), jnp.float32),
                pltpu.VMEM((CORES * used, hid), jnp.float32),
                pltpu.VMEM((CORES * used, hid), bf16),
                pltpu.VMEM((CHUNKS, n_expert, slots, cols), bf16),
                pltpu.VMEM((CHUNKS, n_expert, slots, cols), bf16),
                pltpu.VMEM((CHUNKS, n_expert, slots, cols), bf16),
                pltpu.VMEM((CHUNKS, n_line, tok, cols), bf16),
                pltpu.VMEM((CHUNKS, n_line, tok, cols), bf16),
                dma((3, CHUNKS)),
                dma((n_line - 1,)), dma((n_line - 1,)),
                dma(line), dma(line),
                dma(plane), dma(plane),
                dma((CHUNKS, n_expert)), dma((CHUNKS, n_expert)),
                dma((CHUNKS,)), dma((CHUNKS,)),
                dma(plane), dma(plane),
                dma(line), dma(line),
            ],
            compiler_params=pltpu.CompilerParams(
                collective_id=0, has_side_effects=True, vmem_limit_bytes=67043328
            ),
        )(tokens, norm_gain[None], routes, gate_weights, capacity, w_gate, w_up, w_down)

    return jax.shard_map(
        on_device,
        mesh=mesh,
        in_specs=(
            P(("expert", "shard"), None), P(), P(("expert", "shard"), None), P(("expert", "shard"), None), P(),
            P("expert", None, "shard"), P("expert", None, "shard"), P("expert", "shard", None),
        ),
        out_specs=P(("expert", "shard"), None),
        check_vma=False,
    )
```

time: 145 us -> 53 us (0.37)
  blocking collectives: 74.7 us -> 0 us
  Pallas kernels: 0 us -> 48.6 us
  waiting for transfers between devices: 25 us -> 0 us
  matrix products: 23.1 us -> 0 us
  between operations: 13.5 us -> 0.01 us
  other arithmetic: 5.17 us -> 0 us
    all_to_all x3 -> x0, blocking collectives: 74.7 us -> none  [the longest x1 40.4 us: on_device(): lax.all_to_all(lax.all_to_all(rounded_parts, 'expert', split_axis=1, conc...]
    pallas_call x0 -> x1, Pallas kernels: none -> 48.6 us  [on_device(): pl.pallas_call(functools.partial(kernel, n_expert, n_line, depth), out_sh...]
    all_gather x1 -> x0, waiting for transfers between devices: 25 us -> none  [on_device(): slot_rows = lax.all_gather(arrived[None], 'shard', axis=0, tiled=True)]
    dot_general x5 -> x0, matrix products: 23.1 us -> none  [the longest x1 7.91 us: on_device(): partial_out = jnp.dot(hidden, down_proj, preferred_element_type=jnp.float32)]
    unnamed x0 -> x3, local copies, waits for them, and re-layouts: none -> 4.23 us
    reduce_sum x5 -> x0, other arithmetic: 3.62 us -> none  [the longest x1 1.06 us: rms_norm(): mean_square = jnp.mean(widened * widened, axis=-1, keepdims=True)]
    reshape x1 -> x0, local copies, waits for them, and re-layouts: 2.68 us -> none  [on_device(): flat_rows = slot_rows.reshape(-1, row_shape[-1])]
  transfers between devices with their start and end apart: 1 -> 0, of which waited for: 1 -> 0; matrix products, arithmetic and copies ran while one was open for 0% -> 0% of each run, Pallas kernels for 0% -> 0%
where the time goes in v1:
time: 53 us; the launch traced here: 52.8 us
  Pallas kernels  48.6 us (92%)
  local copies, waits for them, and re-layouts  4.23 us (8%)
    pallas_call x1, Pallas kernels, on_device(): pl.pallas_call(functools.partial(kernel, n_expert, n_line, depth), out_sh...  48.6 us
    unnamed x3, local copies, waits for them, and re-layouts  4.23 us

profile of v1, /device:TPU:0, one launch (start us, length us, event | category | flops | bytes accessed | tf_op | source)
XLA Modules:
  0.0 52.8 jit_solution(4818760547705851692)
XLA Ops:
  0.0 1.3 %copy.9.routes = s32[8,2]{1,0:T(8,128)} copy(s32[8,2]{0,1:T(2,128)} %param.10) | data formatting | bytes 128 | tf_op args[2]
  1.3 1.3 %copy.10.gates = f32[8,2]{1,0:T(8,128)} copy(f32[8,2]{0,1:T(2,128)} %param.11) | data formatting | bytes 128 | tf_op args[3]
  2.7 48.6 %shard_map.82 = bf16[8,6144]{1,0:T(8,128)(2,1)} custom-call(bf16[8,6144]{1,0:T(8,128)(2,1)} %tokens.1, f32[1,6144]{1,0:T(1,128)} %bitcast.1, s32[8,2]{1,0:T(8,128)} %copy.9.routes, f32[8,2]{1,0:T(8,128)} %copy.10.gates, s32[4]{0:T(128)} %capacity.1, bf16[1,6144,1024]{2,1,0:T(8,128)(2,1)} %gate_hbm.1, bf16[1,6144,1024]{2,1,0:T(8,128)(2,1)} %up_hbm.1, ...), custom_call_target="tpu_custom_call" | custom-call | tf_op jit(solution)/shard_map/pallas_call | solution.py:292
  51.3 1.5 %copy.12 = bf16[8,6144]{1,0:T(8,128)(2,1)} copy(bf16[8,6144]{1,0:T(8,128)(2,1)} %shard_map.82) | data formatting | bytes 196608

commit v2 on v1

--- a/solution.py
+++ b/solution.py
@@ -7,7 +7,7 @@
 from jax.experimental.pallas import tpu as pltpu
 from jax.sharding import PartitionSpec as P
 
-CHUNKS = 4
+CHUNKS = 3
 EPS = 1e-05
 MESH = pl.DeviceIdType.MESH
 CORES = 2
@@ -76,13 +76,18 @@
     row = lax.broadcasted_iota(jnp.int32, (tok, lanes), 0)
     lane_expert = lane // slots
     lane_slot = lax.rem(lane, depth)
-    first = routes[:, 0:1] == lane_expert
-    named = first.astype(jnp.float32)
-    weight = jnp.where(first, gates[:, 0:1], 0.0)
-    for k in range(1, routes.shape[1]):
-        this = routes[:, k : k + 1] == lane_expert
-        named = jnp.maximum(named, this.astype(jnp.float32))
-        weight = jnp.where(this, gates[:, k : k + 1], weight)
+    diagonal = lax.broadcasted_iota(jnp.int32, (tok, tok), 0) == lax.broadcasted_iota(jnp.int32, (tok, tok), 1)
+
+    def column(ref, k):
+        return jnp.sum(jnp.where(diagonal, ref[k : k + 1, :].astype(jnp.float32), 0.0), axis=1, keepdims=True)
+
+    expert_of_lane = lane_expert.astype(jnp.float32)
+    named = jnp.zeros((tok, lanes), jnp.float32)
+    weight = jnp.zeros((tok, lanes), jnp.float32)
+    for k in range(routes.shape[0]):
+        this = column(routes, k) == expert_of_lane
+        named = jnp.where(this, 1.0, named)
+        weight = jnp.where(this, column(gates, k), weight)
     rank = jnp.zeros((tok, lanes), jnp.float32)
     for t in range(tok - 1):
         rank = rank + jnp.where(row > t, named[t : t + 1, :], 0.0)
@@ -322,7 +327,7 @@
             compiler_params=pltpu.CompilerParams(
                 collective_id=0, has_side_effects=True, vmem_limit_bytes=67043328
             ),
-        )(tokens, norm_gain[None], routes, gate_weights, capacity, w_gate, w_up, w_down)
+        )(tokens, norm_gain[None], routes.T, gate_weights.T, capacity, w_gate, w_up, w_down)
 
     return jax.shard_map(
         on_device,

time: 53 us -> 49.1 us (0.926)
  local copies, waits for them, and re-layouts: 4.23 us -> 1.54 us
  Pallas kernels: 48.6 us -> 47.4 us
    unnamed x3 -> x1, local copies, waits for them, and re-layouts: 4.23 us -> 1.54 us
    pallas_call x1, Pallas kernels: 48.6 us -> 47.4 us  [on_device(): pl.pallas_call(functools.partial(kernel, n_expert, n_line, depth), out_sh...]
where the time goes in v2:
time: 49.1 us; the launch traced here: 49 us
  Pallas kernels  47.4 us (97%)
  local copies, waits for them, and re-layouts  1.54 us (3%)
    pallas_call x1, Pallas kernels, on_device(): pl.pallas_call(functools.partial(kernel, n_expert, n_line, depth), out_sh...  47.4 us
    unnamed x1, local copies, waits for them, and re-layouts  1.54 us

profile of v2, /device:TPU:0, one launch (start us, length us, event | category | flops | bytes accessed | tf_op | source)
XLA Modules:
  0.0 49.0 jit_solution(16481837705746955319)
XLA Ops:
  0.0 47.4 %shard_map.82 = bf16[8,6144]{1,0:T(8,128)(2,1)} custom-call(bf16[8,6144]{1,0:T(8,128)(2,1)} %tokens.1, f32[1,6144]{1,0:T(1,128)} %bitcast.3, s32[2,8]{1,0:T(2,128)} %bitcast.4, f32[2,8]{1,0:T(2,128)} %bitcast.5, s32[4]{0:T(128)} %capacity.1, bf16[1,6144,1024]{2,1,0:T(8,128)(2,1)} %gate_hbm.1, bf16[1,6144,1024]{2,1,0:T(8,128)(2,1)} %up_hbm.1, ...), custom_call_target="tpu_custom_call" | custom-call | tf_op jit(solution)/shard_map/pallas_call | solution.py:297
  47.4 1.5 %copy.10 = bf16[8,6144]{1,0:T(8,128)(2,1)} copy(bf16[8,6144]{1,0:T(8,128)(2,1)} %shard_map.82) | data formatting | bytes 196608
